TPU v7x, 32 devices: a whole 2x2x4 slice. The times are simulated.
32 devices in a mesh: row: 4 (over y, x), col: 8 (over z, core).
Axes of the slice: x: 2, y: 2, z: 4, core: 2. Of those that a mesh axis runs over, the one named last changes fastest.
Arguments:
- gate_weight: bfloat16 [4608, 36864], P('row', 'col'), may hold values from -8.838835 to 8.838835
- up_weight: bfloat16 [4608, 36864], P('row', 'col'), may hold values from -8.838835 to 8.838835
- routes: int32 [2, 4], replicated, may hold values from 0 to 3, each once within a row
Outputs:
- gate_serving: bfloat16 [4608, 36864], P('col', 'row')
- up_serving: bfloat16 [4608, 36864], P('col', 'row')
- scales: float32 [2, 36864], P(None, 'row')
Inputs may be any that keep to these rules, and one draw needn't show every extreme that they name: Each row of routes names every serving rank's piece once.
All inputs are finite; a program needn't handle non-finite values. Where the computation divides by a largest or mean magnitude, that divisor is 1e-20 or more.
Results may differ from a plain program's by a relative error of at most 0.001.
Values may be sent and summed in bfloat16 or wider, within the bound.
A program may use at most 128 MiB of HBM per device.

v0:
```python
import jax
import jax.numpy as jnp
from jax import lax
from jax.sharding import PartitionSpec as P

EPSILON = 1e-06
LIMIT = 4.0


def column_peaks(weight):
    return jnp.max(jnp.abs(weight), axis=0).astype(jnp.float32)


def quantize(weight, peaks):
    factor = LIMIT / (peaks + EPSILON)
    return (weight.astype(jnp.float32) * factor[None, :]).astype(jnp.bfloat16)


def order_pieces(weight, order, pieces):
    height, width = weight.shape
    shaped = weight.reshape(height, pieces, width // pieces)
    return jnp.take(shaped, order, axis=1).reshape(height, width)


def own_piece(peaks, pick, pieces):
    shaped = ((peaks + EPSILON) / LIMIT).reshape(pieces, -1)
    return lax.dynamic_index_in_dim(shaped, pick, 0, keepdims=False)


def shards(gate_weight, up_weight, routes):
    pieces = lax.axis_size("row")
    row_index = lax.axis_index("row")
    gate_peaks, up_peaks = lax.pmax((column_peaks(gate_weight), column_peaks(up_weight)), "row")
    gate_sent = order_pieces(quantize(gate_weight, gate_peaks), routes[0], pieces)
    up_sent = order_pieces(quantize(up_weight, up_peaks), routes[1], pieces)
    gate_serving, up_serving = (
        lax.all_to_all(
            lax.all_to_all(gate_sent, "row", split_axis=1, concat_axis=0, tiled=True),
            "col",
            split_axis=0,
            concat_axis=1,
            tiled=True,
        ),
        lax.all_to_all(
            lax.all_to_all(up_sent, "row", split_axis=1, concat_axis=0, tiled=True),
            "col",
            split_axis=0,
            concat_axis=1,
            tiled=True,
        ),
    )
    chosen = jnp.take(routes, row_index, axis=1)
    local_scales = jnp.stack(
        [own_piece(gate_peaks, chosen[0], pieces), own_piece(up_peaks, chosen[1], pieces)]
    )
    scales = lax.all_gather(local_scales, "col", axis=1, tiled=True)
    return (gate_serving, up_serving, scales)


def solution(mesh):
    return jax.shard_map(
        shards,
        mesh=mesh,
        in_specs=(P("row", "col"), P("row", "col"), P()),
        out_specs=(P("col", "row"), P("col", "row"), P(None, "row")),
        check_vma=False,
    )
```

profile of v0, /device:TPU:27, one launch (start us, length us, event | category | flops | bytes accessed | tf_op | source)
XLA Modules:
  0.0 833.9 jit_solution(6411490724367084619)
XLA Ops:
  0.6 15.2 %copy.6 = bf16[1152,4608]{0,1:T(8,128)(2,1)} copy(bf16[1152,4608]{1,0:T(8,128)(2,1)} %param.5) | data formatting | bytes 21233664 | tf_op args[0]
  15.8 0.0 copy-start
  15.8 5.2 abs_reduce_fusion.1
  21.1 1.8 copy-done
  22.9 1.1 abs_reduce_fusion
  23.9 11.1 %all-reduce = (f32[4608]{0:T(1024)S(1)}, f32[4608]{0:T(1024)S(1)}) all-reduce(bf16[4608]{0:T(1024)(128)(2,1)S(1)} %abs_reduce_fusion.1, bf16[4608]{0:T(1024)(128)(2,1)S(1)} %abs_reduce_fusion), channel_id=1, replica_groups=mesh['row'=4,'col'=8] {'row'}, use_global_device_ids=true, to_apply=%region_1.0 | all-reduce | flops 9216 | bytes 55296 | tf_op jit(solution)/shard_map/pmax | solution.py:33
  35.1 6.5 multiply_convert_fusion.1
  41.6 2.7 mini-gather-slice.9
  44.3 0.0 copy-start.1
  44.3 3.1 mini-gather-slice.8
  47.3 6.8 copy.15
  54.1 0.0 copy-done.1
  54.1 8.9 %copy.14 = bf16[640,4,1152]{2,0,1:T(8,128)(2,1)} copy(bf16[640,4,1152]{0,2,1:T(8,128)(2,1)} %mini-gather-slice.8) | data formatting | bytes 11796480
  63.0 5.6 gather_fusion.1
  68.6 6.4 gather_fusion
  75.0 10.5 %maximum_select_fusion = bf16[1152,4,1152]{2,0,1:T(8,128)(2,1)} fusion(bf16[512,4,1152]{2,0,1:T(8,128)(2,1)} %bitcast.36, bf16[640,4,1152]{2,0,1:T(8,128)(2,1)} %bitcast.34, pred[4]{0:T(512)(128)(4,1)S(1)} %get-tuple-element.25), kind=kLoop, calls=%fused_computation.6 | loop fusion | flops 26542080 | bytes 21233668 | tf_op jit(solution)/shard_map/jit(_take)/select_n | solution.py:22
  85.5 8.0 all-to-all-start
  93.5 15.2 %copy.10 = bf16[1152,4608]{0,1:T(8,128)(2,1)} copy(bf16[1152,4608]{1,0:T(8,128)(2,1)} %param.6) | data formatting | bytes 21233664 | tf_op args[1]
  108.6 6.5 multiply_convert_fusion
  115.1 2.7 mini-gather-slice.11
  117.8 3.1 mini-gather-slice.10
  120.9 6.7 copy.17
  127.6 8.9 %copy.16 = bf16[640,4,1152]{2,0,1:T(8,128)(2,1)} copy(bf16[640,4,1152]{0,2,1:T(8,128)(2,1)} %mini-gather-slice.10) | data formatting | bytes 11796480
  136.5 5.6 gather_fusion.3
  142.1 6.4 gather_fusion.2
  148.5 10.5 %maximum_select_fusion.1 = bf16[1152,4,1152]{2,0,1:T(8,128)(2,1)} fusion(bf16[512,4,1152]{2,0,1:T(8,128)(2,1)} %bitcast.35, bf16[640,4,1152]{2,0,1:T(8,128)(2,1)} %bitcast.33, pred[4]{0:T(512)(128)(4,1)S(1)} %get-tuple-element.17), kind=kLoop, calls=%fused_computation.7 | loop fusion | flops 26542080 | bytes 21233668 | tf_op jit(solution)/shard_map/jit(_take)/select_n | solution.py:22
  159.0 46.1 %all-to-all-done = bf16[1152,4,1152]{2,0,1:T(8,128)(2,1)} async-done(((bf16[1152,4,1152]{2,0,1:T(8,128)(2,1)}), bf16[1152,4,1152]{2,0,1:T(8,128)(2,1)}, u32[]{:S(2)}, u32[]{:S(2)}) %all-to-all-start) | async-done | bytes 10616864 | tf_op jit(solution)/shard_map/all_to_all | solution.py:38
  205.1 126.9 %all_to_all.64 = bf16[1152,4,1152]{2,0,1:T(8,128)(2,1)} all-to-all(bf16[1152,4,1152]{2,0,1:T(8,128)(2,1)} %maximum_select_fusion.1), channel_id=1, replica_groups=mesh['row'=4,'col'=8] {'row'}, dimensions={1} | all-to-all | bytes 21233664 | tf_op jit(solution)/shard_map/all_to_all | solution.py:45
  331.9 237.6 %all_to_all.65 = bf16[8,576,1152]{2,1,0:T(8,128)(2,1)} all-to-all(bf16[8,576,1152]{2,1,0:T(8,128)(2,1)} %bitcast.5), channel_id=1, replica_groups=mesh['row'=4,'col'=8] {'col'}, dimensions={0} | all-to-all | bytes 21233664 | tf_op jit(solution)/shard_map/all_to_all | solution.py:37
  569.5 7.7 all-to-all-start.3
  577.2 0.2 select_reduce_fusion
  577.4 0.6 fusion
  581.9 232.0 %all_gather.3 = f32[2,9216]{1,0:T(2,128)S(1)} all-gather(f32[2,1152]{1,0:T(2,128)S(1)} %pad_maximum_fusion), channel_id=1, replica_groups=mesh['row'=4,'col'=8] {'col'}, dimensions={1}, use_global_device_ids=true | all-gather | bytes 82944 | tf_op jit(solution)/shard_map/all_gather | solution.py:56
  813.9 9.7 %copy.18 = bf16[8,72,8,1152]{3,2,0,1:T(8,128)(2,1)} copy(bf16[8,72,8,1152]{3,2,1,0:T(8,128)(2,1)} %bitcast.32) | data formatting | bytes 21233664 | tf_op jit(solution)/shard_map/all_to_all | solution.py:37
  823.6 0.0 all-to-all-done.3
  823.6 9.7 %copy.19 = bf16[8,72,8,1152]{3,2,0,1:T(8,128)(2,1)} copy(bf16[8,72,8,1152]{3,2,1,0:T(8,128)(2,1)} %bitcast.21) | data formatting | bytes 21233664 | tf_op jit(solution)/shard_map/all_to_all | solution.py:44
  833.2 0.6 copy.21
  (9 shorter events, 0.1 us)
Async XLA Ops:
  15.8 7.0 copy-start
  44.3 9.8 %copy-start.1 = (s32[2,4]{1,0:T(2,128)S(1)}, s32[2,4]{1,0:T(2,128)}, u32[]{:S(2)}) copy-start(s32[2,4]{1,0:T(2,128)} %param.7) | copy-start | bytes 100
  85.5 119.6 %all-to-all-start = ((bf16[1152,4,1152]{2,0,1:T(8,128)(2,1)}), bf16[1152,4,1152]{2,0,1:T(8,128)(2,1)}, u32[]{:S(2)}, u32[]{:S(2)}) async-start(bf16[1152,4,1152]{2,0,1:T(8,128)(2,1)} %maximum_select_fusion), calls=%async_computation | async-start | bytes 21233664 | tf_op jit(solution)/shard_map/all_to_all | solution.py:38
  569.5 254.1 %all-to-all-start.3 = ((bf16[8,576,1152]{2,1,0:T(8,128)(2,1)}), bf16[8,576,1152]{2,1,0:T(8,128)(2,1)}, u32[]{:S(2)}, u32[]{:S(2)}) async-start(bf16[8,576,1152]{2,1,0:T(8,128)(2,1)} %bitcast.31), calls=%async_computation.3 | async-start | bytes 21233664 | tf_op jit(solution)/shard_map/all_to_all | solution.py:44
where the time goes:
time: 839 us; the launch traced here: 834 us
  blocking collectives  608 us (72%)
  local copies, waits for them, and re-layouts  119 us (14%)
  waiting for transfers between devices  46.1 us (5%)
  other arithmetic  40.5 us (5%)
  starting transfers between devices  15.6 us (2%)
    all_to_all x1, blocking collectives, shards(): lax.all_to_all(lax.all_to_all(gate_sent, 'row', split_axis=1, concat_axis...  238 us
    all_gather x1, blocking collectives, shards(): scales = lax.all_gather(local_scales, 'col', axis=1, tiled=True)  232 us
    all_to_all x1, blocking collectives, shards(): lax.all_to_all(up_sent, 'row', split_axis=1, concat_axis=0, tiled=True)  127 us
    unnamed x11, local copies, waits for them, and re-layouts  64.1 us
    all_to_all x1, waiting for transfers between devices, shards(): lax.all_to_all(gate_sent, 'row', split_axis=1, concat_axis=0, tiled=True)  46.1 us
    gather x8, local copies, waits for them, and re-layouts, order_pieces(): return jnp.take(shaped, order, axis=1).reshape(height, width)  35.4 us
    select_n x2, other arithmetic, order_pieces(): return jnp.take(shaped, order, axis=1).reshape(height, width)  21 us
  transfers between devices with their start and end apart: 2, of which 1 were waited for; matrix products, arithmetic and copies ran while one was open for 9% of the time, Pallas kernels for 0%

commit v1 on v0

v1 whole, which is shorter than its diff:
```python
import functools

import jax
import jax.numpy as jnp
from jax import lax
from jax.experimental import pallas as pl
from jax.experimental.pallas import tpu as pltpu
from jax.sharding import PartitionSpec as P

EPSILON = 1e-06
LIMIT = 4.0
MESH = pl.DeviceIdType.MESH
VMEM_BYTES = 60 * 1024 * 1024
CHUNKS = 4
AHEAD = 2


def column_peaks(weight):
    return jnp.max(jnp.abs(weight), axis=0).astype(jnp.float32)


def quantize(weight, peaks):
    factor = LIMIT / (peaks + EPSILON)
    return (weight.astype(jnp.float32) * factor[None, :]).astype(jnp.bfloat16)


def order_pieces(weight, order, pieces):
    height, width = weight.shape
    shaped = weight.reshape(height, pieces, width // pieces)
    return jnp.take(shaped, order, axis=1).reshape(height, width)


def own_piece(peaks, pick, pieces):
    shaped = ((peaks + EPSILON) / LIMIT).reshape(pieces, -1)
    return lax.dynamic_index_in_dim(shaped, pick, 0, keepdims=False)


def exchange(sent):
    sent = lax.all_to_all(sent, "row", split_axis=1, concat_axis=0, tiled=True)
    return lax.all_to_all(sent, "col", split_axis=0, concat_axis=1, tiled=True)


def plain_shards(gate_weight, up_weight, routes):
    pieces = lax.axis_size("row")
    row_index = lax.axis_index("row")
    gate_peaks, up_peaks = lax.pmax((column_peaks(gate_weight), column_peaks(up_weight)), "row")
    gate_serving = exchange(order_pieces(quantize(gate_weight, gate_peaks), routes[0], pieces))
    up_serving = exchange(order_pieces(quantize(up_weight, up_peaks), routes[1], pieces))
    chosen = jnp.take(routes, row_index, axis=1)
    local_scales = jnp.stack(
        [own_piece(gate_peaks, chosen[0], pieces), own_piece(up_peaks, chosen[1], pieces)]
    )
    scales = lax.all_gather(local_scales, "col", axis=1, tiled=True)
    return (gate_serving, up_serving, scales)


def order_kernel(routes_ref, gate_ref, up_ref, sent_ref, peak_ref):
    @pl.when(pl.program_id(1) == 0)
    def _():
        peak_ref[...] = jnp.zeros_like(peak_ref)

    for p, ref in enumerate((gate_ref, up_ref)):
        block = ref[...]
        sent_ref[0, p] = block
        top = jnp.max(jnp.abs(block.astype(jnp.float32)), axis=0)
        peak_ref[0, p, :] = jnp.maximum(peak_ref[0, p, :], top)


def order_call(gate_weight, up_weight, routes, n_row, steps):
    height, width = gate_weight.shape
    piece, tile = width // n_row, height // steps
    return pl.pallas_call(
        order_kernel,
        grid_spec=pltpu.PrefetchScalarGridSpec(
            num_scalar_prefetch=1,
            grid=(n_row, steps),
            in_specs=[
                pl.BlockSpec((tile, piece), lambda i, j, routes: (j, routes[0, i])),
                pl.BlockSpec((tile, piece), lambda i, j, routes: (j, routes[1, i])),
            ],
            out_specs=[
                pl.BlockSpec((1, 2, tile, piece), lambda i, j, routes: (i, 0, j, 0)),
                pl.BlockSpec((1, 2, piece), lambda i, j, routes: (i, 0, 0)),
            ],
        ),
        out_shape=[
            jax.ShapeDtypeStruct((n_row, 2, height, piece), gate_weight.dtype),
            jax.ShapeDtypeStruct((n_row, 2, piece), jnp.float32),
        ],
    )(routes, gate_weight, up_weight)


def move_kernel(
    n_row, n_col, depth, parts,
    sent_ref, peak_ref, got_ref, peaks_ref,
    mid, peak_mid, peak_own,
    send1, recv1, send2, recv2, psend1, precv1, psend2, precv2,
):
    row, col = lax.axis_index("row"), lax.axis_index("col")
    ratio = n_col // n_row
    size = depth // parts
    total = 2 * ratio * parts

    barrier = pltpu.get_barrier_semaphore()
    for s in range(1, n_row):
        pl.semaphore_signal(
            barrier, inc=1, device_id=(lax.rem(row + s, n_row), col), device_id_type=MESH
        )
    for s in range(1, n_col):
        pl.semaphore_signal(
            barrier, inc=1, device_id=(row, lax.rem(col + s, n_col)), device_id_type=MESH
        )
    pl.semaphore_wait(barrier, n_row + n_col - 2)

    def place(k):
        p, rest = k // (ratio * parts), k % (ratio * parts)
        q, h = rest // ratio, rest % ratio
        src = pl.ds(pl.multiple_of((p * ratio + h) * depth + q * size, 16), size)
        dst = pl.ds(pl.multiple_of(p * depth + q * size, 16), size)
        return h, p * parts + q, src, dst

    def first(k, s):
        _, _, src, _ = place(k)
        to = lax.rem(row + s, n_row)
        return pltpu.make_async_remote_copy(
            src_ref=sent_ref.at[to, src],
            dst_ref=mid.at[n_row - 1 - s, src],
            send_sem=send1.at[k, s - 1],
            recv_sem=recv1.at[k, s - 1],
            device_id=(to, col),
            device_id_type=MESH,
        )

    def second(k, s):
        h, slot, src, dst = place(k)
        source = lax.rem(row + n_row - s, n_row)
        to = source * ratio + h
        block = sent_ref.at[row, src] if s == 0 else mid.at[n_row - 1 - s, src]
        remote = pltpu.make_async_remote_copy(
            src_ref=block,
            dst_ref=got_ref.at[col, dst],
            send_sem=send2.at[k, s],
            recv_sem=recv2.at[slot, col],
            device_id=(row, to),
            device_id_type=MESH,
        )
        local = pltpu.make_async_copy(block, got_ref.at[col, dst], recv2.at[slot, col])
        return to, remote, local

    def start_second(k, s):
        to, remote, local = second(k, s)

        @pl.when(to != col)
        def _():
            remote.start()

        @pl.when(to == col)
        def _():
            local.start()

    def peak_first(s):
        to = lax.rem(row + s, n_row)
        return pltpu.make_async_remote_copy(
            src_ref=peak_ref.at[to],
            dst_ref=peak_mid.at[s - 1],
            send_sem=psend1.at[s - 1],
            recv_sem=precv1.at[s - 1],
            device_id=(to, col),
            device_id_type=MESH,
        )

    def peak_second(s):
        return pltpu.make_async_remote_copy(
            src_ref=peak_own,
            dst_ref=peaks_ref.at[col],
            send_sem=psend2.at[s - 1],
            recv_sem=precv2.at[s - 1],
            device_id=(row, lax.rem(col + s, n_col)),
            device_id_type=MESH,
        )

    def begin(k):
        for s in range(1, n_row):
            first(k, s).start()
        start_second(k, 0)

    for s in range(1, n_row):
        peak_first(s).start()
    for k in range(AHEAD):
        begin(k)
    top = peak_ref[row]
    for s in range(1, n_row):
        peak_first(s).wait_recv()
        top = jnp.maximum(top, peak_mid[s - 1])
    peak_own[...] = top
    peaks_ref[col] = top

    @pl.loop(0, total)
    def _(k):
        @pl.when(k + AHEAD < total)
        def _():
            begin(k + AHEAD)

        for s in range(1, n_row):
            first(k, s).wait_recv()
            start_second(k, s)

    for s in range(1, n_col):
        peak_second(s).start()

    @pl.loop(0, total)
    def _(k):
        for s in range(1, n_row):
            first(k, s).wait_send()
        for s in range(n_row):
            to, remote, _ = second(k, s)

            @pl.when(to != col)
            def _():
                remote.wait_send()

    for s in range(1, n_row):
        peak_first(s).wait_send()
    for s in range(1, n_col):
        peak_second(s).wait()

    @pl.loop(0, 2 * parts)
    def _(slot):
        for c in range(n_col):
            block = got_ref.at[c, pl.ds(pl.multiple_of(slot * size, 16), size)]
            pltpu.make_async_copy(block, block, recv2.at[slot, c]).wait()


def move_call(sent, peaks, n_row, n_col, parts):
    piece = sent.shape[-1]
    ratio = n_col // n_row
    depth = sent.shape[1] // (2 * ratio)
    total = 2 * ratio * parts
    dma = pltpu.SemaphoreType.DMA
    return pl.pallas_call(
        functools.partial(move_kernel, n_row, n_col, depth, parts),
        out_shape=[
            jax.ShapeDtypeStruct((n_col, 2 * depth, piece), sent.dtype),
            jax.ShapeDtypeStruct((n_col, 2, piece), jnp.float32),
        ],
        in_specs=[
            pl.BlockSpec(memory_space=pl.ANY),
            pl.BlockSpec(memory_space=pltpu.VMEM),
        ],
        out_specs=[
            pl.BlockSpec(memory_space=pl.ANY),
            pl.BlockSpec(memory_space=pltpu.VMEM),
        ],
        scratch_shapes=[
            pltpu.VMEM((n_row - 1, 2 * ratio * depth, piece), sent.dtype),
            pltpu.VMEM((n_row - 1, 2, piece), jnp.float32),
            pltpu.VMEM((2, piece), jnp.float32),
            dma((total, n_row - 1)),
            dma((total, n_row - 1)),
            dma((total, n_row)),
            dma((2 * parts, n_col)),
            dma((n_row - 1,)),
            dma((n_row - 1,)),
            dma((n_col - 1,)),
            dma((n_col - 1,)),
        ],
        compiler_params=pltpu.CompilerParams(
            collective_id=0, has_side_effects=True, vmem_limit_bytes=VMEM_BYTES
        ),
    )(sent, peaks)


def finish_kernel(got_ref, peaks_ref, gate_ref, up_ref, scales_ref):
    base = peaks_ref[0] + EPSILON
    scales_ref[...] = base / LIMIT
    factor = LIMIT / base
    for p, ref in enumerate((gate_ref, up_ref)):
        block = got_ref[0, p].astype(jnp.float32)
        ref[...] = (block * factor[p][None, :]).astype(ref.dtype)


def finish_call(got, peaks, steps):
    n_col, _, depth, piece = got.shape
    tile = depth // steps
    return pl.pallas_call(
        finish_kernel,
        grid=(n_col, steps),
        in_specs=[
            pl.BlockSpec((1, 2, tile, piece), lambda c, j: (c, 0, j, 0)),
            pl.BlockSpec((1, 2, piece), lambda c, j: (c, 0, 0)),
        ],
        out_specs=[
            pl.BlockSpec((tile, piece), lambda c, j: (j, c)),
            pl.BlockSpec((tile, piece), lambda c, j: (j, c)),
            pl.BlockSpec((2, piece), lambda c, j: (0, c)),
        ],
        out_shape=[
            jax.ShapeDtypeStruct((depth, n_col * piece), got.dtype),
            jax.ShapeDtypeStruct((depth, n_col * piece), got.dtype),
            jax.ShapeDtypeStruct((2, n_col * piece), jnp.float32),
        ],
    )(got, peaks)


def kernel_shards(n_row, n_col, gate_weight, up_weight, routes):
    height, width = gate_weight.shape
    piece = width // n_row
    sent, peaks = order_call(gate_weight, up_weight, routes, n_row, 4)
    sent = sent.reshape(n_row, 2 * height, piece)
    got, tops = move_call(sent, peaks, n_row, n_col, CHUNKS)
    got = got.reshape(n_col, 2, height * n_row // n_col, piece)
    return tuple(finish_call(got, tops, 2))


def fits(n_row, n_col, height, width):
    if n_col % n_row or width % n_row or (width // n_row) % 128:
        return False
    ratio = n_col // n_row
    mid_bytes = (n_row - 1) * 2 * height * (width // n_row) * 2
    return height % (ratio * CHUNKS * 16) == 0 and mid_bytes < 48 * 1024 * 1024


def solution(mesh):
    n_row, n_col = mesh.shape["row"], mesh.shape["col"]

    def shards(gate_weight, up_weight, routes):
        if fits(n_row, n_col, *gate_weight.shape):
            return kernel_shards(n_row, n_col, gate_weight, up_weight, routes)
        return plain_shards(gate_weight, up_weight, routes)

    return jax.shard_map(
        shards,
        mesh=mesh,
        in_specs=(P("row", "col"), P("row", "col"), P()),
        out_specs=(P("col", "row"), P("col", "row"), P(None, "row")),
        check_vma=False,
    )
```

time: 839 us -> 521 us (0.62)
  blocking collectives: 608 us -> 0 us
  Pallas kernels: 0 us -> 519 us
  local copies, waits for them, and re-layouts: 119 us -> 0 us
  waiting for transfers between devices: 46.1 us -> 0 us
  other arithmetic: 40.5 us -> 0 us
  starting transfers between devices: 15.6 us -> 0 us
    pallas_call x0 -> x3, Pallas kernels: none -> 519 us  [the longest x1 478 us: move_call(): pl.pallas_call(functools.partial(move_kernel, n_row, n_col, depth, parts)...]
    all_to_all x2 -> x0, blocking collectives: 364 us -> none  [the longest x1 238 us: shards(): lax.all_to_all(lax.all_to_all(gate_sent, 'row', split_axis=1, concat_axis...]
    all_gather x1 -> x0, blocking collectives: 232 us -> none  [shards(): scales = lax.all_gather(local_scales, 'col', axis=1, tiled=True)]
    unnamed x11 -> x0, local copies, waits for them, and re-layouts: 64.1 us -> none
    all_to_all x2 -> x0, waiting for transfers between devices: 46.1 us -> none  [the longest x1 46.1 us: shards(): lax.all_to_all(gate_sent, 'row', split_axis=1, concat_axis=0, tiled=True)]
    gather x8 -> x0, local copies, waits for them, and re-layouts: 35.4 us -> none  [order_pieces(): return jnp.take(shaped, order, axis=1).reshape(height, width)]
    select_n x3 -> x0, other arithmetic: 21.1 us -> none  [the longest x2 21 us: order_pieces(): return jnp.take(shaped, order, axis=1).reshape(height, width)]
    all_to_all x2 -> x0, local copies, waits for them, and re-layouts: 19.3 us -> none  [the longest x1 9.65 us: shards(): lax.all_to_all(lax.all_to_all(up_sent, 'row', split_axis=1, concat_axis=0...]
  transfers between devices with their start and end apart: 2 -> 0, of which waited for: 1 -> 0; matrix products, arithmetic and copies ran while one was open for 9% -> 0% of each run, Pallas kernels for 0% -> 0%
where the time goes in v1:
time: 521 us; the launch traced here: 520 us
  Pallas kernels  519 us (100%)
    pallas_call x1, Pallas kernels, move_call(): pl.pallas_call(functools.partial(move_kernel, n_row, n_col, depth, parts)...  478 us
    pallas_call x1, Pallas kernels, order_call(): pl.pallas_call(order_kernel, grid_spec=pltpu.PrefetchScalarGridSpec(num_s...  21.3 us
    pallas_call x1, Pallas kernels, finish_call(): pl.pallas_call(finish_kernel, grid=(n_col, steps), in_specs=[pl.BlockSpec...  20.1 us

profile of v1, /device:TPU:27, one launch (start us, length us, event | category | flops | bytes accessed | tf_op | source)
XLA Modules:
  0.0 519.8 jit_solution(4803680171346330363)
XLA Ops:
  0.6 21.3 %shard_map.58 = (bf16[4,2,1152,1152]{3,2,1,0:T(8,128)(2,1)}, f32[4,2,1152]{2,1,0:T(2,128)}) custom-call(s32[2,4]{1,0:T(2,128)} %routes_ref.1, bf16[1152,4608]{1,0:T(8,128)(2,1)} %gate_ref.1, bf16[1152,4608]{1,0:T(8,128)(2,1)} %up_ref.1), custom_call_target="tpu_custom_call" | custom-call | tf_op jit(solution)/shard_map/pallas_call | solution.py:72
  21.9 477.7 %shard_map.59 = (bf16[8,1152,1152]{2,1,0:T(8,128)(2,1)}, f32[8,2,1152]{2,1,0:T(2,128)}) custom-call(bf16[4,2304,1152]{2,1,0:T(8,128)(2,1)} %bitcast.3, f32[4,2,1152]{2,1,0:T(2,128)} %get-tuple-element.8.peak_ref), custom_call_target="tpu_custom_call" | custom-call | tf_op jit(solution)/shard_map/pallas_call | solution.py:240
  499.6 20.1 %shard_map.60 = (bf16[576,9216]{1,0:T(8,128)(2,1)}, bf16[576,9216]{1,0:T(8,128)(2,1)}, f32[2,9216]{1,0:T(2,128)}) custom-call(bf16[8,2,576,1152]{3,2,1,0:T(8,128)(2,1)} %bitcast.2, f32[8,2,1152]{2,1,0:T(2,128)} %get-tuple-element.10.peaks_ref), custom_call_target="tpu_custom_call" | custom-call | tf_op jit(solution)/shard_map/pallas_call | solution.py:285

commit v2 on v1

--- a/solution.py
+++ b/solution.py
@@ -54,52 +54,17 @@
     return (gate_serving, up_serving, scales)
 
 
-def order_kernel(routes_ref, gate_ref, up_ref, sent_ref, peak_ref):
-    @pl.when(pl.program_id(1) == 0)
-    def _():
-        peak_ref[...] = jnp.zeros_like(peak_ref)
-
-    for p, ref in enumerate((gate_ref, up_ref)):
-        block = ref[...]
-        sent_ref[0, p] = block
-        top = jnp.max(jnp.abs(block.astype(jnp.float32)), axis=0)
-        peak_ref[0, p, :] = jnp.maximum(peak_ref[0, p, :], top)
-
-
-def order_call(gate_weight, up_weight, routes, n_row, steps):
-    height, width = gate_weight.shape
-    piece, tile = width // n_row, height // steps
-    return pl.pallas_call(
-        order_kernel,
-        grid_spec=pltpu.PrefetchScalarGridSpec(
-            num_scalar_prefetch=1,
-            grid=(n_row, steps),
-            in_specs=[
-                pl.BlockSpec((tile, piece), lambda i, j, routes: (j, routes[0, i])),
-                pl.BlockSpec((tile, piece), lambda i, j, routes: (j, routes[1, i])),
-            ],
-            out_specs=[
-                pl.BlockSpec((1, 2, tile, piece), lambda i, j, routes: (i, 0, j, 0)),
-                pl.BlockSpec((1, 2, piece), lambda i, j, routes: (i, 0, 0)),
-            ],
-        ),
-        out_shape=[
-            jax.ShapeDtypeStruct((n_row, 2, height, piece), gate_weight.dtype),
-            jax.ShapeDtypeStruct((n_row, 2, piece), jnp.float32),
-        ],
-    )(routes, gate_weight, up_weight)
-
-
 def move_kernel(
     n_row, n_col, depth, parts,
-    sent_ref, peak_ref, got_ref, peaks_ref,
-    mid, peak_mid, peak_own,
-    send1, recv1, send2, recv2, psend1, precv1, psend2, precv2,
+    routes_ref, gate_ref, up_ref, got_ref, peaks_ref,
+    rows, sent_ref, mid, tops, peak_ref, peak_mid, peak_own,
+    load, send1, recv1, send2, recv2, psend1, precv1, psend2, precv2,
 ):
     row, col = lax.axis_index("row"), lax.axis_index("col")
     ratio = n_col // n_row
     size = depth // parts
     total = 2 * ratio * parts
+    piece = gate_ref.shape[1] // n_row
 
     barrier = pltpu.get_barrier_semaphore()
     for s in range(1, n_row):
@@ -179,48 +144,119 @@
             device_id_type=MESH,
         )
 
+    def fetch(k, ref):
+        _, _, src, _ = place(k)
+        height = ratio * depth
+        start = pl.multiple_of(lax.rem(src.start, height), 16)
+        slot = lax.rem(k, 2)
+        return pltpu.make_async_copy(ref.at[pl.ds(start, size)], rows.at[slot], load.at[slot])
+
+    def start_fetch(k):
+        @pl.when(k < total // 2)
+        def _():
+            fetch(k, gate_ref).start()
+
+        @pl.when(k >= total // 2)
+        def _():
+            fetch(k, up_ref).start()
+
+    def pick(p, i, pieces):
+        chosen = pieces[0]
+        for j in range(1, n_row):
+            chosen = jnp.where(routes_ref[p, i] == j, pieces[j], chosen)
+        return chosen
+
+    def prepare(k):
+        fetch(k, gate_ref).wait()
+        p, slot = k // (ratio * parts), lax.rem(k, 2)
+        _, _, src, _ = place(k)
+
+        @pl.loop(0, size // 16)
+        def _(g):
+            here = pl.ds(pl.multiple_of(g * 16, 16), 16)
+            there = pl.ds(pl.multiple_of(src.start + g * 16, 16), 16)
+            pieces = [rows[slot, here, pl.ds(j * piece, piece)] for j in range(n_row)]
+            for j in range(n_row):
+                cols = pl.ds(j * piece, piece)
+                tops[p, :, cols] = jnp.maximum(tops[p, :, cols], jnp.abs(pieces[j]))
+            for i in range(n_row):
+                sent_ref[i, there, :] = pick(p, i, pieces)
+
+        @pl.when(k + 2 < total)
+        def _():
+            start_fetch(k + 2)
+
     def begin(k):
         for s in range(1, n_row):
             first(k, s).start()
         start_second(k, 0)
 
-    for s in range(1, n_row):
-        peak_first(s).start()
+    tops[...] = jnp.zeros_like(tops)
+    start_fetch(0)
+    start_fetch(1)
+    prepare(0)
     for k in range(AHEAD):
+        prepare(k + 1)
         begin(k)
-    top = peak_ref[row]
-    for s in range(1, n_row):
-        peak_first(s).wait_recv()
-        top = jnp.maximum(top, peak_mid[s - 1])
-    peak_own[...] = top
-    peaks_ref[col] = top
 
     @pl.loop(0, total)
     def _(k):
+        @pl.when(k + AHEAD + 1 < total)
+        def _():
+            prepare(k + AHEAD + 1)
+
         @pl.when(k + AHEAD < total)
         def _():
             begin(k + AHEAD)
+
+        @pl.when(k == total - AHEAD - 1)
+        def _():
+            for p in range(2):
+                pieces = [
+                    jnp.max(tops[p, :, pl.ds(j * piece, piece)].astype(jnp.float32), axis=0, keepdims=True)
+                    for j in range(n_row)
+                ]
+                for i in range(n_row):
+                    peak_ref[i, pl.ds(p, 1), :] = pick(p, i, pieces)
 
         for s in range(1, n_row):
             first(k, s).wait_recv()
             start_second(k, s)
 
-    for s in range(1, n_col):
-        peak_second(s).start()
+    def drain(k):
+        for s in range(n_row):
+            to, remote, _ = second(k, s)
+
+            @pl.when(to != col)
+            def _():
+                remote.wait_send()
+
+    for s in range(1, n_row):
+        peak_first(s).start()
 
     @pl.loop(0, total)
     def _(k):
         for s in range(1, n_row):
             first(k, s).wait_send()
-        for s in range(n_row):
-            to, remote, _ = second(k, s)
-
-            @pl.when(to != col)
-            def _():
-                remote.wait_send()
-
+
+    top = peak_ref[row]
     for s in range(1, n_row):
-        peak_first(s).wait_send()
+        peak_first(s).wait()
+        top = jnp.maximum(top, peak_mid[s - 1])
+    peak_own[...] = top
+    peaks_ref[col] = top
+
+    @pl.loop(0, total * 3 // 4)
+    def _(k):
+        drain(k)
+
+    for s in range(1, n_col):
+        peak_second(s).start()
+
+    @pl.loop(total * 3 // 4, total)
+    def _(k):
+        drain(k)
+
     for s in range(1, n_col):
         peak_second(s).wait()
 
@@ -231,30 +267,38 @@
             pltpu.make_async_copy(block, block, recv2.at[slot, c]).wait()
 
 
-def move_call(sent, peaks, n_row, n_col, parts):
-    piece = sent.shape[-1]
+def move_call(gate_weight, up_weight, routes, n_row, n_col, parts):
+    height, width = gate_weight.shape
+    kind = gate_weight.dtype
+    piece = width // n_row
     ratio = n_col // n_row
-    depth = sent.shape[1] // (2 * ratio)
+    depth = height // ratio
     total = 2 * ratio * parts
     dma = pltpu.SemaphoreType.DMA
     return pl.pallas_call(
         functools.partial(move_kernel, n_row, n_col, depth, parts),
         out_shape=[
-            jax.ShapeDtypeStruct((n_col, 2 * depth, piece), sent.dtype),
+            jax.ShapeDtypeStruct((n_col, 2 * depth, piece), kind),
             jax.ShapeDtypeStruct((n_col, 2, piece), jnp.float32),
         ],
         in_specs=[
+            pl.BlockSpec(memory_space=pltpu.SMEM),
             pl.BlockSpec(memory_space=pl.ANY),
-            pl.BlockSpec(memory_space=pltpu.VMEM),
+            pl.BlockSpec(memory_space=pl.ANY),
         ],
         out_specs=[
             pl.BlockSpec(memory_space=pl.ANY),
             pl.BlockSpec(memory_space=pltpu.VMEM),
         ],
         scratch_shapes=[
-            pltpu.VMEM((n_row - 1, 2 * ratio * depth, piece), sent.dtype),
+            pltpu.VMEM((2, depth // parts, width), kind),
+            pltpu.VMEM((n_row, 2 * height, piece), kind),
+            pltpu.VMEM((n_row - 1, 2 * height, piece), kind),
+            pltpu.VMEM((2, 16, width), kind),
+            pltpu.VMEM((n_row, 2, piece), jnp.float32),
             pltpu.VMEM((n_row - 1, 2, piece), jnp.float32),
             pltpu.VMEM((2, piece), jnp.float32),
+            dma((2,)),
             dma((total, n_row - 1)),
             dma((total, n_row - 1)),
             dma((total, n_row)),
@@ -267,7 +311,7 @@
         compiler_params=pltpu.CompilerParams(
             collective_id=0, has_side_effects=True, vmem_limit_bytes=VMEM_BYTES
         ),
-    )(sent, peaks)
+    )(routes, gate_weight, up_weight)
 
 
 def finish_kernel(got_ref, peaks_ref, gate_ref, up_ref, scales_ref):
@@ -303,21 +347,19 @@
 
 
 def kernel_shards(n_row, n_col, gate_weight, up_weight, routes):
-    height, width = gate_weight.shape
-    piece = width // n_row
-    sent, peaks = order_call(gate_weight, up_weight, routes, n_row, 4)
-    sent = sent.reshape(n_row, 2 * height, piece)
-    got, tops = move_call(sent, peaks, n_row, n_col, CHUNKS)
+    height = gate_weight.shape[0]
+    got, tops = move_call(gate_weight, up_weight, routes, n_row, n_col, CHUNKS)
+    piece = got.shape[-1]
     got = got.reshape(n_col, 2, height * n_row // n_col, piece)
-    return tuple(finish_call(got, tops, 2))
+    return tuple(finish_call(got, tops, 1))
 
 
 def fits(n_row, n_col, height, width):
     if n_col % n_row or width % n_row or (width // n_row) % 128:
         return False
     ratio = n_col // n_row
-    mid_bytes = (n_row - 1) * 2 * height * (width // n_row) * 2
-    return height % (ratio * CHUNKS * 16) == 0 and mid_bytes < 48 * 1024 * 1024
+    held_bytes = (2 * n_row - 1) * 2 * height * (width // n_row) * 2
+    return height % (ratio * CHUNKS * 16) == 0 and held_bytes < 48 * 1024 * 1024
 
 
 def solution(mesh):

time: 521 us -> 497 us (0.954)
  Pallas kernels: 519 us -> 496 us
    pallas_call x1 -> x0, Pallas kernels: 21.3 us -> none  [order_call(): pl.pallas_call(order_kernel, grid_spec=pltpu.PrefetchScalarGridSpec(num_s...]
where the time goes in v2:
time: 497 us; the launch traced here: 496 us
  Pallas kernels  496 us (100%)
    pallas_call x1, Pallas kernels, move_call(): pl.pallas_call(functools.partial(move_kernel, n_row, n_col, depth, parts)...  479 us
    pallas_call x1, Pallas kernels, finish_call(): pl.pallas_call(finish_kernel, grid=(n_col, steps), in_specs=[pl.BlockSpec...  16.3 us

profile of v2, /device:TPU:27, one launch (start us, length us, event | category | flops | bytes accessed | tf_op | source)
XLA Modules:
  0.0 496.4 jit_solution(8729396680844833015)
XLA Ops:
  0.6 479.4 %shard_map.58 = (bf16[8,1152,1152]{2,1,0:T(8,128)(2,1)}, f32[8,2,1152]{2,1,0:T(2,128)}) custom-call(s32[2,4]{1,0:T(2,128)} %routes_ref.1, bf16[1152,4608]{1,0:T(8,128)(2,1)} %gate_ref.1, bf16[1152,4608]{1,0:T(8,128)(2,1)} %up_ref.1), custom_call_target="tpu_custom_call" | custom-call | tf_op jit(solution)/shard_map/pallas_call | solution.py:278
  480.1 16.3 %shard_map.59 = (bf16[576,9216]{1,0:T(8,128)(2,1)}, bf16[576,9216]{1,0:T(8,128)(2,1)}, f32[2,9216]{1,0:T(2,128)}) custom-call(bf16[8,2,576,1152]{3,2,1,0:T(8,128)(2,1)} %bitcast.1, f32[8,2,1152]{2,1,0:T(2,128)} %get-tuple-element.6.peaks_ref), custom_call_target="tpu_custom_call" | custom-call | tf_op jit(solution)/shard_map/pallas_call | solution.py:329
